TPU v7x, 32 devices: a whole 2x2x4 slice. The times are simulated.
32 devices in a mesh: grp: 4 (over z), dev: 8 (over y, x, core).
Axes of the slice: x: 2, y: 2, z: 4, core: 2. Of those that a mesh axis runs over, the one named last changes fastest.
Arguments:
- amounts: float32 [64, 524288], P('dev', 'grp'), may hold values from -0.06 to 0.06, as said below
Outputs:
- offsets: float32 [64, 524288], P(None, ('grp', 'dev'))
Inputs may be any that keep to these rules, and one draw needn't show every extreme that they name: `amounts`: each entry lies within 0.06 of zero.
All inputs are finite; a program needn't handle non-finite values.
Results may differ from a plain program's by a relative error of at most 0.00095.
Values sent between devices are 32-bit elements; how exact they have to be, the bound alone decides.
A program may use at most 64 MiB of HBM per device.

v0:
```python
import functools

import jax
import jax.numpy as jnp
from jax import lax
from jax.experimental import pallas as pl
from jax.experimental.pallas import tpu as pltpu
from jax.sharding import PartitionSpec as P

MESH = pl.DeviceIdType.MESH
LANES = 128
VMEM_GRANT = 46 << 20


def partner(me, k, n):
    if n & (n - 1):
        return lax.rem(me + k, n)
    other, bit = me, 1
    while bit < n:
        if k & bit:
            other = other + bit - 2 * bit * lax.rem(me // bit, 2)
        bit *= 2
    return other


def visit_order(n):
    return [*range(2, n, 2), *range(3, n, 2), *range(1, min(n, 2)), 0]


def greeting(n):
    if n & (n - 1) or n < 8:
        return list(range(1, n)), []
    across = (1 << (n.bit_length() - 2) // 2) - 1 << 1
    down = n - 2 - across
    near = [k for k in range(1, n) if not (k & across and k & down)]
    return near, [k for k in near if not k & (down | 1)]


def piece_spans(rows):
    cuts = [0, rows // 8, rows // 2, rows]
    return list(zip(cuts[:-1], cuts[1:]))


def kernel(n, groups, x_ref, t_ref, carry_ref, x_vm, s_vm, w_vm, run_vm, group_vm, give_vm,
           load_sem, send_sem, recv_sem, rsend_sem, rrecv_sem, csend_sem, crecv_sem, zsend_sem, zrecv_sem, ready_sem):
    me, grp = lax.axis_index("dev"), lax.axis_index("grp")
    chans, rows = t_ref.shape[1:]
    order = visit_order(n)
    spans = piece_spans(rows)
    others = {k: partner(me, k, n) for k in order}

    barrier = pltpu.get_barrier_semaphore()
    near, relays = greeting(n)
    for k in near:
        pl.semaphore_signal(barrier, inc=1, device_id={"dev": partner(me, k, n)}, device_id_type=MESH)

    @pl.when(grp > 0)
    def _():
        pl.semaphore_signal(barrier, inc=1, device_id={"grp": grp - 1}, device_id_type=MESH)

    @pl.when(grp < groups - 1)
    def _():
        pl.semaphore_signal(barrier, inc=1, device_id={"grp": grp + 1}, device_id_type=MESH)

    def load(piece, k):
        lo, hi = spans[piece]
        at = pl.ds(pl.multiple_of(others[k] * rows + lo, LANES), hi - lo)
        return pltpu.make_async_copy(x_ref.at[:, at], x_vm.at[:, at], load_sem.at[piece, k])

    for piece in range(len(spans)):
        for k in order:
            load(piece, k).start()

    shape = (2 * LANES, 2 * LANES)
    tile = min(rows // 8, 2048)
    steps = tile // LANES

    def scan(source, base, lo, hi, dest, run):
        def one(i, run):
            start = lo + i * tile
            block = source[:, pl.ds(pl.multiple_of(base + start, LANES), tile)]
            stack = jnp.concatenate(
                [block[:, j * LANES:(j + 1) * LANES] for j in range(steps)], axis=0)
            high = stack.astype(jnp.bfloat16)
            rest = stack - high.astype(jnp.float32)
            mid = rest.astype(jnp.bfloat16)
            low = (rest - mid.astype(jnp.float32)).astype(jnp.bfloat16)
            sums = jnp.dot(jnp.concatenate([high, mid], axis=1), w_vm[...],
                           preferred_element_type=jnp.float32)
            sums = sums + jnp.dot(low, w_vm[:LANES, :], preferred_element_type=jnp.float32)
            for j in range(steps):
                part = sums[j * chans:(j + 1) * chans]
                at = pl.ds(pl.multiple_of(start + j * LANES, LANES), LANES)
                dest[:, at] = part[:, :LANES] + run
                run = run + part[:, LANES:]
            return run

        return lax.fori_loop(0, (hi - lo) // tile, one, run)

    def raw(k, source):
        at = pl.ds(pl.multiple_of(others[k] * rows, LANES), spans[0][1])
        return pltpu.make_async_remote_copy(
            src_ref=x_vm.at[:, at], dst_ref=t_ref.at[source, :, pl.ds(0, spans[0][1])],
            send_sem=rsend_sem.at[others[k]], recv_sem=rrecv_sem.at[source],
            device_id={"dev": others[k]}, device_id_type=MESH)

    def send(piece, k):
        lo, hi = spans[piece]
        at = pl.ds(lo, hi - lo)
        pltpu.make_async_remote_copy(
            src_ref=s_vm.at[others[k], :, at], dst_ref=t_ref.at[me, :, at],
            send_sem=send_sem.at[others[k]], recv_sem=recv_sem.at[me],
            device_id={"dev": others[k]}, device_id_type=MESH).start()

    chained = jnp.where(grp > 0, 1, 0) + jnp.where(grp < groups - 1, 1, 0)
    pl.semaphore_wait(barrier, len(near) + chained)
    for k in relays:
        pl.semaphore_signal(ready_sem, inc=1, device_id={"dev": partner(me, k, n)}, device_id_type=MESH)
    met = False
    for k in [*(k for k in order if k in near), *(k for k in order if k not in near)]:
        if relays and not met and k not in near:
            pl.semaphore_wait(ready_sem, len(relays))
            met = True
        load(0, k).wait()
        if k:
            raw(k, me).start()

    row = lax.rem(lax.broadcasted_iota(jnp.int32, shape, 0), LANES)
    col = lax.broadcasted_iota(jnp.int32, shape, 1)
    w_vm[...] = jnp.where((row < col) | (col >= LANES), 1.0, 0.0).astype(jnp.bfloat16)
    run_vm[...] = jnp.zeros_like(run_vm)

    late = None
    for piece in range(len(spans)):
        for k in order:
            if piece:
                load(piece, k).wait()
            dest = s_vm.at[others[k]] if k else t_ref.at[me]
            run_vm[others[k]] = scan(x_vm, others[k] * rows, *spans[piece], dest, run_vm[others[k]])
            if late is not None:
                send(*late)
            late = (piece, k) if k and piece else None

    total = jnp.zeros((chans, LANES), jnp.float32)
    for j in range(n):
        give_vm[j] = total
        total = total + run_vm[j]

    def pass_on():
        return pltpu.make_async_remote_copy(
            src_ref=group_vm.at[1], dst_ref=group_vm.at[0], send_sem=zsend_sem, recv_sem=zrecv_sem,
            device_id={"grp": grp + 1}, device_id_type=MESH)

    @pl.when(grp == 0)
    def _():
        group_vm[0] = jnp.zeros_like(total)

    @pl.when(grp > 0)
    def _():
        pass_on().wait_recv()

    before = group_vm[0]
    group_vm[1] = before + total
    for j in range(n):
        give_vm[j] = give_vm[j] + before
    carry_ref[me] = give_vm[me]

    @pl.when(grp < groups - 1)
    def _():
        pass_on().start()

    def give(k, source):
        return pltpu.make_async_remote_copy(
            src_ref=give_vm.at[others[k]], dst_ref=carry_ref.at[source],
            send_sem=csend_sem.at[others[k]], recv_sem=crecv_sem.at[source],
            device_id={"dev": others[k]}, device_id_type=MESH)

    for k in order:
        if k:
            give(k, me).start()

    @pl.when(grp < groups - 1)
    def _():
        pass_on().wait_send()

    for k in order:
        if k:
            raw(k, others[k]).wait()
            block = t_ref.at[others[k]]
            scan(block, 0, *spans[0], block, jnp.zeros((chans, LANES), jnp.float32))

    rest = pl.ds(spans[0][1], rows - spans[0][1])
    for k in order:
        if k:
            pltpu.make_async_remote_copy(
                src_ref=s_vm.at[others[k], :, rest], dst_ref=t_ref.at[others[k], :, rest],
                send_sem=send_sem.at[others[k]], recv_sem=recv_sem.at[others[k]],
                device_id={"dev": others[k]}, device_id_type=MESH).wait()
            give(k, others[k]).wait()


def finish(n, t_ref, carry_ref, out_ref, stage, sem):
    rows = t_ref.shape[2]
    step = min(rows, 16 * LANES)

    def copy(j):
        return pltpu.make_async_copy(stage.at[j], out_ref.at[j], sem.at[j])

    for j in range(n):
        carry = carry_ref[j]
        wide = jnp.concatenate([carry] * (step // LANES), axis=1)

        def add(i, _):
            at = pl.ds(pl.multiple_of(i * step, LANES), step)
            stage[j, :, at] = t_ref[j, :, at] + wide
            return 0

        lax.fori_loop(0, rows // step, add, 0, unroll=True)
        copy(j).start()
    for j in range(n):
        copy(j).wait()


def solution(mesh):
    n, groups = mesh.shape["dev"], mesh.shape["grp"]

    def local(amounts):
        chans, length = amounts.shape
        rows = length // n
        f32 = jnp.float32
        table, carry = pl.pallas_call(
            functools.partial(kernel, n, groups),
            out_shape=[jax.ShapeDtypeStruct((n, chans, rows), f32),
                       jax.ShapeDtypeStruct((n, chans, LANES), f32)],
            in_specs=[pl.BlockSpec(memory_space=pl.ANY)],
            out_specs=[pl.BlockSpec(memory_space=pltpu.VMEM)] * 2,
            scratch_shapes=[
                pltpu.VMEM((chans, length), f32),
                pltpu.VMEM((n, chans, rows), f32),
                pltpu.VMEM((2 * LANES, 2 * LANES), jnp.bfloat16),
                pltpu.VMEM((n, chans, LANES), f32),
                pltpu.VMEM((2, chans, LANES), f32),
                pltpu.VMEM((n, chans, LANES), f32),
                pltpu.SemaphoreType.DMA((len(piece_spans(rows)), n)),
                pltpu.SemaphoreType.DMA((n,)),
                pltpu.SemaphoreType.DMA((n,)),
                pltpu.SemaphoreType.DMA((n,)),
                pltpu.SemaphoreType.DMA((n,)),
                pltpu.SemaphoreType.DMA((n,)),
                pltpu.SemaphoreType.DMA((n,)),
                pltpu.SemaphoreType.DMA,
                pltpu.SemaphoreType.DMA,
                pltpu.SemaphoreType.REGULAR,
            ],
            compiler_params=pltpu.CompilerParams(
                collective_id=0, has_side_effects=True, vmem_limit_bytes=VMEM_GRANT),
            name="exchange",
        )(amounts)
        out = pl.pallas_call(
            functools.partial(finish, n),
            out_shape=jax.ShapeDtypeStruct((n, chans, rows), f32),
            in_specs=[pl.BlockSpec(memory_space=pltpu.VMEM)] * 2,
            out_specs=pl.BlockSpec(memory_space=pl.ANY),
            scratch_shapes=[
                pltpu.VMEM((n, chans, rows), f32),
                pltpu.SemaphoreType.DMA((n,)),
            ],
            compiler_params=pltpu.CompilerParams(vmem_limit_bytes=VMEM_GRANT),
            name="finish",
        )(table, carry)
        return out.reshape(n * chans, rows)

    return jax.shard_map(
        local,
        mesh=mesh,
        in_specs=(P("dev", "grp"),),
        out_specs=P(None, ("grp", "dev")),
        check_vma=False,
    )
```

profile of v0, /device:TPU:0, one launch (start us, length us, event | category | flops | bytes accessed | tf_op | source)
XLA Modules:
  0.0 54.1 jit_solution(12306894303513050060)
XLA Ops:
  0.0 51.9 %exchange.1 = (f32[8,8,16384]{2,1,0:T(8,128)S(1)}, f32[8,8,128]{2,1,0:T(8,128)S(1)}) custom-call(f32[8,131072]{1,0:T(8,128)} %x_ref.1), custom_call_target="tpu_custom_call" | custom-call | tf_op jit(solution)/shard_map/exchange/pallas_call | solution.py:231
  51.9 2.1 %finish.1 = f32[8,8,16384]{2,1,0:T(8,128)} custom-call(f32[8,8,16384]{2,1,0:T(8,128)S(1)} %get-tuple-element.7.t_ref, f32[8,8,128]{2,1,0:T(8,128)S(1)} %get-tuple-element.8.carry_ref), custom_call_target="tpu_custom_call" | custom-call | tf_op jit(solution)/shard_map/finish/pallas_call | solution.py:259
where the time goes:
time: 54.2 us; the launch traced here: 54.1 us
  Pallas kernels  54 us (100%)
    pallas_call x1, Pallas kernels, local(): pl.pallas_call(functools.partial(kernel, n, groups), out_shape=[jax.Shape...  51.9 us
    pallas_call x1, Pallas kernels, local(): pl.pallas_call(functools.partial(finish, n), out_shape=jax.ShapeDtypeStru...  2.11 us

commit v1 on v0

v1 whole, which is shorter than its diff:
```python
import functools

import jax
import jax.numpy as jnp
from jax import lax
from jax.experimental import pallas as pl
from jax.experimental.pallas import tpu as pltpu
from jax.sharding import PartitionSpec as P

MESH = pl.DeviceIdType.MESH
LANES = 128
VMEM_GRANT = 46 << 20


def flip(me, k):
    other, bit = me, 1
    while bit <= k:
        if k & bit:
            other = other + bit - 2 * bit * lax.rem(me // bit, 2)
        bit *= 2
    return other


def classes(n):
    across = (1 << (n.bit_length() - 2) // 2) - 1 << 1
    down = n - 2 - across
    order = sorted(range(2, n), key=lambda k: (k & 1, k))
    xs = [k for k in order if not k & down]
    ys = [k for k in order if not k & across]
    ds = [k for k in order if k & across and k & down]
    return across, xs, ys, ds


def tile_of(rows):
    return min(rows // 8, 2048)


def scan_tile(block, w_ref, run):
    chans, tile = block.shape
    steps = tile // LANES
    stack = jnp.concatenate([block[:, j * LANES:(j + 1) * LANES] for j in range(steps)], axis=0)
    high = stack.astype(jnp.bfloat16)
    rest = stack - high.astype(jnp.float32)
    mid = rest.astype(jnp.bfloat16)
    low = (rest - mid.astype(jnp.float32)).astype(jnp.bfloat16)
    sums = jnp.dot(jnp.concatenate([high, mid], axis=1), w_ref[...], preferred_element_type=jnp.float32)
    sums = sums + jnp.dot(low, w_ref[:LANES, :], preferred_element_type=jnp.float32)
    parts = []
    for j in range(steps):
        part = sums[j * chans:(j + 1) * chans]
        parts.append(part[:, :LANES] + run)
        run = run + part[:, LANES:]
    return parts, run


def exchange(n, groups, x_ref, t_ref, run_ref, w_ref, x_vm, relay_vm, give_vm, carry_vm, group_vm,
             load_sem, send_sem, recv_sem, hsend_sem, hrecv_sem, csend_sem, crecv_sem, zsend_sem, zrecv_sem,
             note_sem, ready_sem, zready_sem):
    me, grp = lax.axis_index("dev"), lax.axis_index("grp")
    core = lax.rem(me, 2)
    base = me - core
    chans, rows = t_ref.shape[1:]
    tile = tile_of(rows)
    across, xs, ys, ds = classes(n)
    late = (xs[-1], ds[-1])
    others = {k: flip(me, k) for k in range(n)}
    x_chips = [k for k in xs if not k & 1]
    y_chips = [k for k in ys if not k & 1]

    def signal(sem, **device):
        pl.semaphore_signal(sem, inc=1, device_id=device, device_id_type=MESH)

    barrier = pltpu.get_barrier_semaphore()
    for k in y_chips:
        signal(barrier, dev=flip(base, k) + 1)
    for k in x_chips:
        signal(barrier, dev=flip(base, k))

    @pl.when(core == 1)
    def _():
        signal(barrier, dev=base)

    @pl.when(grp > 0)
    def _():
        signal(barrier, grp=grp - 1, dev=0)

    def part(k, lo, size):
        return pl.ds(pl.multiple_of(others[k] * rows + lo, LANES), size)

    def load(k):
        return pltpu.make_async_copy(x_ref.at[:, part(k, 0, rows)], x_vm.at[:, part(k, 0, rows)], load_sem.at[k])

    for pair in zip(ys, ds):
        for k in pair:
            load(k).start()
    for k in [*ys[len(ds):], *ds[len(ys):], *xs, 1, 0]:
        load(k).start()

    def spans(k):
        cuts = [0, rows // 2, rows - tile, rows] if k in late else [0, rows]
        return list(enumerate(zip(cuts[:-1], cuts[1:])))

    def direct(k, piece, lo, hi, source):
        return pltpu.make_async_remote_copy(
            src_ref=x_vm.at[:, part(k, lo, hi - lo)], dst_ref=t_ref.at[source, :, pl.ds(lo, hi - lo)],
            send_sem=send_sem.at[piece, others[k]], recv_sem=recv_sem.at[piece, source],
            device_id={"dev": others[k]}, device_id_type=MESH)

    def hop(k):
        slot = ds.index(k)
        return pltpu.make_async_remote_copy(
            src_ref=x_vm.at[:, part(k, 0, rows)], dst_ref=relay_vm.at[slot],
            send_sem=hsend_sem.at[slot], recv_sem=hrecv_sem.at[slot],
            device_id={"dev": others[k & across]}, device_id_type=MESH)

    def relay(k, piece, lo, hi, source):
        slot = ds.index(k)
        return pltpu.make_async_remote_copy(
            src_ref=relay_vm.at[slot, :, pl.ds(lo, hi - lo)], dst_ref=t_ref.at[source, :, pl.ds(lo, hi - lo)],
            send_sem=send_sem.at[piece, others[k]], recv_sem=recv_sem.at[piece, source],
            device_id={"dev": others[k & ~across]}, device_id_type=MESH)

    def send(ks):
        for k in ks:
            load(k).wait()
            for piece, (lo, hi) in spans(k):
                direct(k, piece, lo, hi, me).start()

    def send_hops():
        for k in ds:
            load(k).wait()
            hop(k).start()

    @pl.when(core == 0)
    def _():
        after = jnp.where((me == 0) & (grp < groups - 1), n, 0)
        pl.semaphore_wait(barrier, 1 + 2 * len(x_chips) + after)
        signal(note_sem, dev=base + 1)
        send_hops()
        pl.semaphore_wait(note_sem, 1)
        send(ys)

    @pl.when(core == 1)
    def _():
        pl.semaphore_wait(barrier, 2 * len(y_chips))
        send(ys)
        pl.semaphore_wait(note_sem, 1)
        signal(note_sem, dev=base)
        for k in x_chips:
            signal(ready_sem, dev=flip(base, k))
            signal(ready_sem, dev=flip(base, k) + 1)
        send_hops()

    send([1])
    for k in [*xs, 0]:
        load(k).wait()

    shape = (2 * LANES, 2 * LANES)
    row = lax.rem(lax.broadcasted_iota(jnp.int32, shape, 0), LANES)
    col = lax.broadcasted_iota(jnp.int32, shape, 1)
    w_ref[...] = jnp.where((row < col) | (col >= LANES), 1.0, 0.0).astype(jnp.bfloat16)

    def range_total(j, total):
        give_vm[j] = total

        def one(i, acc):
            block = x_vm[:, pl.ds(pl.multiple_of(j * rows + i * tile, LANES), tile)]
            parts = [block[:, s * LANES:(s + 1) * LANES] for s in range(tile // LANES)]
            while len(parts) > 1:
                parts = [a + b for a, b in zip(parts[::2], parts[1::2])] + parts[len(parts) & ~1:]
            return acc + parts[0]

        acc = lax.fori_loop(0, rows // tile, one, jnp.zeros((chans, LANES), jnp.float32))
        return total + jnp.broadcast_to(jnp.sum(acc, axis=1, keepdims=True), acc.shape)

    total = lax.fori_loop(0, n, range_total, jnp.zeros((chans, LANES), jnp.float32))

    pl.semaphore_wait(ready_sem, len(x_chips))

    @pl.when((me == 0) & (grp < groups - 1))
    def _():
        for k in range(1, n):
            signal(zready_sem, dev=k)

    def pass_on():
        return pltpu.make_async_remote_copy(
            src_ref=group_vm.at[1], dst_ref=group_vm.at[0], send_sem=zsend_sem, recv_sem=zrecv_sem,
            device_id={"grp": grp + 1}, device_id_type=MESH)

    @pl.when((me > 0) & (grp < groups - 1))
    def _():
        pl.semaphore_wait(zready_sem, 1)

    @pl.when(grp == 0)
    def _():
        group_vm[0] = jnp.zeros_like(total)

    @pl.when(grp > 0)
    def _():
        pass_on().wait_recv()

    before = group_vm[0]
    group_vm[1] = before + total
    for j in range(n):
        give_vm[j] = give_vm[j] + before
    carry_vm[me] = give_vm[me]

    @pl.when(grp < groups - 1)
    def _():
        pass_on().start()

    def give(k, source):
        return pltpu.make_async_remote_copy(
            src_ref=give_vm.at[others[k]], dst_ref=carry_vm.at[source],
            send_sem=csend_sem.at[others[k]], recv_sem=crecv_sem.at[source],
            device_id={"dev": others[k]}, device_id_type=MESH)

    for k in [1, *ys, *xs, *ds]:
        give(k, me).start()
    for k in xs:
        for piece, (lo, hi) in spans(k):
            direct(k, piece, lo, hi, me).start()

    def scan(source, start, dest, lo, hi, run):
        def one(i, run):
            parts, run = scan_tile(source[:, pl.ds(pl.multiple_of(start + lo + i * tile, LANES), tile)], w_ref, run)
            for j, sums in enumerate(parts):
                dest[:, pl.ds(pl.multiple_of(lo + i * tile + j * LANES, LANES), LANES)] = sums
            return run

        return lax.fori_loop(0, (hi - lo) // tile, one, run)

    scan(x_vm, me * rows, t_ref.at[me], 0, rows, carry_vm[me])

    def arrived(k, piece, lo, hi):
        copy = relay if k in ds else direct
        copy(k, piece, lo, hi, others[k]).wait_recv()

    def finish(k):
        give(k, others[k]).wait_recv()
        arrived(k, 0, 0, rows)
        block = t_ref.at[others[k]]
        scan(block, 0, block, 0, rows, carry_vm[others[k]])

    finish(1)
    for k in ds:
        hop(k).wait_recv()
        for piece, (lo, hi) in spans(k):
            relay(k, piece, lo, hi, others[k & across]).start()
    for k in ys:
        finish(k)
    rest = [k for pair in zip(xs, ds) for k in pair] + xs[len(ds):] + ds[len(xs):]
    for k in rest:
        if k not in late:
            finish(k)
    runs = {}
    for k in late:
        give(k, others[k]).wait_recv()
        runs[k] = carry_vm[others[k]]
    *early, last = spans(late[0])
    for piece, (lo, hi) in early:
        for k in late:
            arrived(k, piece, lo, hi)
            block = t_ref.at[others[k]]
            runs[k] = scan(block, 0, block, lo, hi, runs[k])
    for i, k in enumerate(late):
        run_ref[i] = runs[k]

    @pl.when(grp < groups - 1)
    def _():
        pass_on().wait_send()

    for k in range(1, n):
        give(k, me).wait_send()
    for k in ds:
        hop(k).wait_send()
    for k in range(1, n):
        for piece, (lo, hi) in spans(k):
            (relay if k in ds else direct)(k, piece, lo, hi, me).wait_send()
    for k in late:
        arrived(k, last[0], *last[1])


def write(n, t_ref, run_ref, w_ref, out_ref, stage, main_sem, last_sem):
    me = lax.axis_index("dev")
    rows = t_ref.shape[2]
    tile = tile_of(rows)
    _, xs, _, ds = classes(n)
    late = (xs[-1], ds[-1])
    main, last = pl.ds(0, rows - tile), pl.ds(rows - tile, tile)

    def whole(k):
        at = flip(me, k)
        if k in late:
            return pltpu.make_async_copy(t_ref.at[at, :, main], out_ref.at[at, :, main], main_sem.at[k])
        return pltpu.make_async_copy(t_ref.at[at], out_ref.at[at], main_sem.at[k])

    def tail(i, k):
        return pltpu.make_async_copy(stage.at[i], out_ref.at[flip(me, k), :, last], last_sem.at[i])

    for k in range(n):
        whole(k).start()
    for i, k in enumerate(late):
        parts, _ = scan_tile(t_ref[flip(me, k), :, last], w_ref, run_ref[i])
        for j, sums in enumerate(parts):
            stage[i, :, pl.ds(j * LANES, LANES)] = sums
        tail(i, k).start()
    for k in range(n):
        whole(k).wait()
    for i, k in enumerate(late):
        tail(i, k).wait()


def solution(mesh):
    n, groups = mesh.shape["dev"], mesh.shape["grp"]
    assert n >= 8 and not n & (n - 1)

    def local(amounts):
        chans, length = amounts.shape
        rows = length // n
        tile = tile_of(rows)
        diagonals = len(classes(n)[3])
        f32 = jnp.float32
        dma = pltpu.SemaphoreType.DMA
        regular = pltpu.SemaphoreType.REGULAR
        wide = (2 * LANES, 2 * LANES)
        table, run, weights = pl.pallas_call(
            functools.partial(exchange, n, groups),
            out_shape=[jax.ShapeDtypeStruct((n, chans, rows), f32),
                       jax.ShapeDtypeStruct((2, chans, LANES), f32),
                       jax.ShapeDtypeStruct(wide, jnp.bfloat16)],
            in_specs=[pl.BlockSpec(memory_space=pl.ANY)],
            out_specs=[pl.BlockSpec(memory_space=pltpu.VMEM)] * 3,
            scratch_shapes=[
                pltpu.VMEM((chans, length), f32),
                pltpu.VMEM((diagonals, chans, rows), f32),
                pltpu.VMEM((n, chans, LANES), f32),
                pltpu.VMEM((n, chans, LANES), f32),
                pltpu.VMEM((2, chans, LANES), f32),
                dma((n,)), dma((3, n)), dma((3, n)), dma((diagonals,)), dma((diagonals,)),
                dma((n,)), dma((n,)), dma, dma, regular, regular, regular,
            ],
            compiler_params=pltpu.CompilerParams(
                collective_id=0, has_side_effects=True, vmem_limit_bytes=VMEM_GRANT),
            name="exchange",
        )(amounts)
        out = pl.pallas_call(
            functools.partial(write, n),
            out_shape=jax.ShapeDtypeStruct((n, chans, rows), f32),
            in_specs=[pl.BlockSpec(memory_space=pltpu.VMEM)] * 3,
            out_specs=pl.BlockSpec(memory_space=pl.ANY),
            scratch_shapes=[pltpu.VMEM((2, chans, tile), f32), dma((n,)), dma((2,))],
            compiler_params=pltpu.CompilerParams(vmem_limit_bytes=VMEM_GRANT),
            name="write",
        )(table, run, weights)
        return out.reshape(n * chans, rows)

    return jax.shard_map(
        local,
        mesh=mesh,
        in_specs=(P("dev", "grp"),),
        out_specs=P(None, ("grp", "dev")),
        check_vma=False,
    )
```

time: 54.2 us -> 54.2 us (level)
  no operation moved by 1% of the time
where the time goes in v1:
time: 54.2 us; the launch traced here: 54 us
  Pallas kernels  54 us (100%)
    pallas_call x1, Pallas kernels, local(): pl.pallas_call(functools.partial(exchange, n, groups), out_shape=[jax.Sha...  51.9 us
    pallas_call x1, Pallas kernels, local(): pl.pallas_call(functools.partial(write, n), out_shape=jax.ShapeDtypeStruc...  2.14 us

profile of v1, /device:TPU:0, one launch (start us, length us, event | category | flops | bytes accessed | tf_op | source)
XLA Modules:
  0.0 54.0 jit_solution(14820859235076505165)
XLA Ops:
  0.0 51.9 %exchange.1 = (f32[8,8,16384]{2,1,0:T(8,128)S(1)}, f32[2,8,128]{2,1,0:T(8,128)S(1)}, bf16[256,256]{1,0:T(8,128)(2,1)S(1)}) custom-call(f32[8,131072]{1,0:T(8,128)} %x_ref.1), custom_call_target="tpu_custom_call" | custom-call | tf_op jit(solution)/shard_map/exchange/pallas_call | solution.py:327
  51.9 2.1 %write.1 = f32[8,8,16384]{2,1,0:T(8,128)} custom-call(f32[8,8,16384]{2,1,0:T(8,128)S(1)} %get-tuple-element.8.t_ref, f32[2,8,128]{2,1,0:T(8,128)S(1)} %get-tuple-element.9.run_ref, bf16[256,256]{1,0:T(8,128)(2,1)S(1)} %get-tuple-element.10.w_ref), custom_call_target="tpu_custom_call" | custom-call | tf_op jit(solution)/shard_map/write/pallas_call | solution.py:347

commit v2 on v1

v2 whole, which is shorter than its diff:
```python
import functools

import jax
import jax.numpy as jnp
from jax import lax
from jax.experimental import pallas as pl
from jax.experimental.pallas import tpu as pltpu
from jax.sharding import PartitionSpec as P

MESH = pl.DeviceIdType.MESH
LANES = 128
VMEM_GRANT = 46 << 20


def flip(me, k):
    other, bit = me, 1
    while bit <= k:
        if k & bit:
            other = other + bit - 2 * bit * lax.rem(me // bit, 2)
        bit *= 2
    return other


def chips(n):
    across = (1 << (n.bit_length() - 2) // 2) - 1 << 1
    flips = range(2, n, 2)
    xs = [k for k in flips if not k & ~across]
    ys = [k for k in flips if not k & across]
    ds = [k for k in flips if k & across and k & ~across]
    return across, xs, ys, ds


def late_flips(n):
    _, xs, _, ds = chips(n)
    return [k + core for k in [*xs, *ds] for core in (0, 1)]


def tile_of(rows):
    return min(rows // 8, 2048)


def cuts_of(rows):
    cuts = [0, rows // 4, rows // 2, 3 * rows // 4, rows - tile_of(rows), rows]
    return list(zip(cuts[:-1], cuts[1:]))


def scan_tiles(blocks, w_ref, runs):
    chans, width = blocks[0].shape
    steps = width // LANES
    stack = jnp.concatenate(
        [block[:, j * LANES:(j + 1) * LANES] for block in blocks for j in range(steps)], axis=0)
    high = stack.astype(jnp.bfloat16)
    rest = stack - high.astype(jnp.float32)
    mid = rest.astype(jnp.bfloat16)
    low = (rest - mid.astype(jnp.float32)).astype(jnp.bfloat16)
    sums = jnp.dot(jnp.concatenate([high, mid], axis=1), w_ref[...], preferred_element_type=jnp.float32)
    sums = sums + jnp.dot(low, w_ref[:LANES, :], preferred_element_type=jnp.float32)
    outs, after = [], []
    for i, run in enumerate(runs):
        parts = []
        for j in range(i * steps, (i + 1) * steps):
            part = sums[j * chans:(j + 1) * chans]
            parts.append(part[:, :LANES] + run)
            run = run + part[:, LANES:]
        outs.append(parts)
        after.append(run)
    return outs, after


def exchange(n, groups, x_ref, t_ref, run_ref, w_ref, x_vm, relay_vm, give_vm, carry_vm, group_vm,
             load_sem, send_sem, recv_sem, hsend_sem, hrecv_sem, csend_sem, crecv_sem, zsend_sem, zrecv_sem,
             note_sem, ready_sem, hello_sem, zready_sem):
    me, grp = lax.axis_index("dev"), lax.axis_index("grp")
    core = lax.rem(me, 2)
    base = me - core
    partner = base + 1 - core
    chans, rows = t_ref.shape[1:]
    tile = tile_of(rows)
    pieces = cuts_of(rows)
    whole = [(0, rows)]
    across, xs, ys, ds = chips(n)
    late = [flip(me, k) for k in late_flips(n)]

    def x_core(chip):
        return jnp.where(lax.rem(chip // 2, across // 2 + 1) > 0, 1, 0)

    def targets(k):
        chip = flip(base, k)
        first = jnp.where((chip == 0) & (grp == 0), 0, 1)
        return [chip + first, chip + 1 - first]

    def signal(sem, **device):
        pl.semaphore_signal(sem, inc=1, device_id=device, device_id_type=MESH)

    barrier = pltpu.get_barrier_semaphore()
    for k in ys:
        signal(barrier, dev=flip(base, k) + 1 - x_core(base))
    for k in xs:
        signal(barrier, dev=flip(base, k) + x_core(flip(base, k)))

    @pl.when(core == 1)
    def _():
        signal(barrier, dev=base)

    @pl.when((me == 0) & (grp > 0))
    def _():
        signal(barrier, grp=grp - 1, dev=0)

    def at(j, lo=0, size=rows):
        return pl.ds(pl.multiple_of(j * rows + lo, LANES), size)

    def load(sem, j, lo=0, size=rows):
        return pltpu.make_async_copy(x_ref.at[:, at(j, lo, size)], x_vm.at[:, at(j, lo, size)], load_sem.at[sem])

    def remote(src, dst, sems, device):
        return pltpu.make_async_remote_copy(
            src_ref=src, dst_ref=dst, send_sem=sems[0], recv_sem=sems[1],
            device_id=device, device_id_type=MESH)

    def direct(j, sem, lo, hi):
        remote(x_vm.at[:, at(j, lo, hi - lo)], t_ref.at[me, :, pl.ds(lo, hi - lo)],
               (send_sem, recv_sem.at[sem]), {"dev": j}).start()

    def hop(j, slot, lo, hi):
        remote(x_vm.at[:, at(j, lo, hi - lo)], relay_vm.at[slot, :, pl.ds(lo, hi - lo)],
               (hsend_sem, hrecv_sem.at[slot]), {"dev": flip(me, ds[slot // 2] & across)}).start()

    def relay(j, slot, sem, lo, hi):
        source = flip(me, ds[slot // 2] & across)
        remote(relay_vm.at[slot, :, pl.ds(lo, hi - lo)], t_ref.at[source, :, pl.ds(lo, hi - lo)],
               (send_sem, recv_sem.at[sem]), {"dev": j}).start()

    x_blocks = [j for k in xs for j in targets(k)]
    y_blocks = [j for k in ys for j in targets(k)]
    d_blocks = [j for k in ds for j in targets(k)]

    def send_y(slots, spans):
        for slot in slots:
            for lo, hi in spans:
                direct(y_blocks[slot], 1, lo, hi)

    def send_d(slots, spans):
        for slot in slots:
            for lo, hi in spans:
                hop(d_blocks[slot], slot, lo, hi)

    turns = [(core == x_core(base), d_blocks, y_blocks, send_d, send_y),
             (core != x_core(base), y_blocks, d_blocks, send_y, send_d)]

    for mine, first, second, _, _ in turns:
        @pl.when(mine)
        def _():
            load(0, first[0], 0, tile).start()
            load(1, first[0], tile, rows - tile).start()
            for j in [*first[1:], *second]:
                load(2, j).start()

    for j in [*x_blocks, me, partner]:
        load(2, j).start()

    after = jnp.where((me == 0) & (grp < groups - 1), 1, 0)
    faced = jnp.where(core == x_core(base), 2 * len(xs), 2 * len(ys))
    pl.semaphore_wait(barrier, faced + 1 - core + after)

    for mine, first, _, send_first, _ in turns:
        @pl.when(mine)
        def _():
            load(0, first[0], 0, tile).wait()
            send_first([0], [(0, tile)])
            load(1, first[0], tile, rows - tile).wait()
            send_first([0], [(tile, rows)])

    @pl.when(core == 0)
    def _():
        signal(note_sem, dev=base + 1)

    @pl.when((me == 0) & (grp < groups - 1))
    def _():
        signal(hello_sem, grp=grp + 1)

    @pl.when(core == 1)
    def _():
        pl.semaphore_wait(note_sem, 1)
        signal(note_sem, dev=base)
        for k in xs:
            signal(ready_sem, dev=flip(base, k))
            signal(ready_sem, dev=flip(base, k) + 1)

    load(2, 0, 0, (n - 1) * rows).wait()
    for mine, first, _, send_first, _ in turns:
        @pl.when(mine)
        def _():
            send_first(range(1, len(first)), whole)

    @pl.when(core == 0)
    def _():
        pl.semaphore_wait(note_sem, 1)

    for mine, _, second, _, send_second in turns:
        @pl.when(mine)
        def _():
            send_second(range(len(second)), whole)

    direct(partner, 0, 0, rows)

    shape = (2 * LANES, 2 * LANES)
    row = lax.rem(lax.broadcasted_iota(jnp.int32, shape, 0), LANES)
    col = lax.broadcasted_iota(jnp.int32, shape, 1)
    w_ref[...] = jnp.where((row < col) | (col >= LANES), 1.0, 0.0).astype(jnp.bfloat16)

    def range_total(j, total):
        give_vm[j] = total

        def one(i, acc):
            block = x_vm[:, at(j, i * tile, tile)]
            parts = [block[:, s * LANES:(s + 1) * LANES] for s in range(tile // LANES)]
            while len(parts) > 1:
                parts = [a + b for a, b in zip(parts[::2], parts[1::2])] + parts[len(parts) & ~1:]
            return acc + parts[0]

        acc = lax.fori_loop(0, rows // tile, one, jnp.zeros((chans, LANES), jnp.float32))
        return total + jnp.broadcast_to(jnp.sum(acc, axis=1, keepdims=True), acc.shape)

    total = lax.fori_loop(0, n, range_total, jnp.zeros((chans, LANES), jnp.float32))

    pl.semaphore_wait(ready_sem, len(xs))

    @pl.when((me == 0) & (grp > 0))
    def _():
        pl.semaphore_wait(hello_sem, 1)
        signal(zready_sem, grp=grp - 1)

    @pl.when(grp < groups - 1)
    def _():
        pl.semaphore_wait(zready_sem, 1)

    @pl.when((me == 0) & (grp < groups - 1))
    def _():
        for k in range(1, n):
            signal(zready_sem, dev=k)

    def pass_on():
        return remote(group_vm.at[1], group_vm.at[0], (zsend_sem, zrecv_sem), {"grp": grp + 1})

    @pl.when(grp == 0)
    def _():
        group_vm[0] = jnp.zeros_like(total)

    @pl.when(grp > 0)
    def _():
        pass_on().wait_recv()

    before = group_vm[0]
    group_vm[1] = before + total
    for j in range(n):
        give_vm[j] = give_vm[j] + before
    carry_vm[me] = give_vm[me]

    @pl.when(grp < groups - 1)
    def _():
        pass_on().start()

    for j in [partner, *y_blocks, *x_blocks, *d_blocks]:
        remote(give_vm.at[j], carry_vm.at[me], (csend_sem, crecv_sem), {"dev": j}).start()
    for j in x_blocks:
        for i, (lo, hi) in enumerate(pieces):
            direct(j, 2 + i, lo, hi)

    def scan(blocks, lo, hi, runs):
        width = min(hi - lo, 4 * tile // len(blocks))

        def one(i, runs):
            start = lo + i * width
            tiles = [source[:, pl.ds(pl.multiple_of(offset + start, LANES), width)] for source, offset, _ in blocks]
            outs, runs = scan_tiles(tiles, w_ref, runs)
            for (_, _, dest), parts in zip(blocks, outs):
                for j, sums in enumerate(parts):
                    dest[:, pl.ds(pl.multiple_of(start + j * LANES, LANES), LANES)] = sums
            return tuple(runs)

        return lax.fori_loop(0, (hi - lo) // width, one, tuple(runs))

    def in_place(j):
        return t_ref.at[j], 0, t_ref.at[j]

    def arrived(sem, blocks, lo=0, hi=rows):
        span = t_ref.at[pl.ds(0, blocks), :, pl.ds(lo, hi - lo)]
        remote(span, span, (send_sem, recv_sem.at[sem]), {"dev": partner}).wait_recv()

    scan([(x_vm, me * rows, t_ref.at[me])], 0, rows, [carry_vm[me]])
    for slot in range(len(d_blocks)):
        remote(relay_vm.at[slot], relay_vm.at[slot], (hsend_sem, hrecv_sem.at[slot]), {"dev": partner}).wait_recv()
        j = targets(ds[slot // 2] & ~across)[slot % 2]
        for i, (lo, hi) in enumerate(pieces):
            relay(j, slot, 2 + i, lo, hi)

    gives = carry_vm.at[pl.ds(0, n - 1)]
    remote(gives, gives, (csend_sem, crecv_sem), {"dev": partner}).wait()
    arrived(0, 1)
    scan([in_place(partner)], 0, rows, [carry_vm[partner]])
    arrived(1, len(y_blocks))
    for s in range(0, len(y_blocks), 2):
        pair = y_blocks[s:s + 2]
        scan([in_place(j) for j in pair], 0, rows, [carry_vm[j] for j in pair])

    for i, j in enumerate(late):
        run_ref[i] = carry_vm[j]
    for i, (lo, hi) in enumerate(pieces[:-1]):
        arrived(2 + i, len(late), lo, hi)
        for s in range(0, len(late), 4):
            four = late[s:s + 4]
            runs = scan([in_place(j) for j in four], lo, hi, [run_ref[s + r] for r in range(len(four))])
            for r, run in enumerate(runs):
                run_ref[s + r] = run

    @pl.when(grp < groups - 1)
    def _():
        pass_on().wait_send()

    remote(relay_vm, relay_vm, (hsend_sem, hrecv_sem.at[0]), {"dev": partner}).wait_send()
    sent = x_vm.at[:, pl.ds(0, (n - 1) * rows)]
    remote(sent, sent, (send_sem, recv_sem.at[0]), {"dev": partner}).wait_send()
    arrived(1 + len(pieces), len(late), *pieces[-1])


def write(n, t_ref, run_ref, w_ref, out_ref, stage, sem):
    me = lax.axis_index("dev")
    rows = t_ref.shape[2]
    tile = tile_of(rows)
    late = late_flips(n)
    main, last = pl.ds(0, rows - tile), pl.ds(rows - tile, tile)

    for k in range(n):
        j = flip(me, k)
        if k in late:
            pltpu.make_async_copy(t_ref.at[j, :, main], out_ref.at[j, :, main], sem).start()
        else:
            pltpu.make_async_copy(t_ref.at[j], out_ref.at[j], sem).start()
    for s in range(0, len(late), 4):
        four = late[s:s + 4]
        outs, _ = scan_tiles([t_ref[flip(me, k), :, last] for k in four], w_ref, [run_ref[s + r] for r in range(len(four))])
        for r, (k, parts) in enumerate(zip(four, outs)):
            for j, sums in enumerate(parts):
                stage[s + r, :, pl.ds(j * LANES, LANES)] = sums
            pltpu.make_async_copy(stage.at[s + r], out_ref.at[flip(me, k), :, last], sem).start()
    pltpu.make_async_copy(t_ref, out_ref, sem).wait()


def solution(mesh):
    n, groups = mesh.shape["dev"], mesh.shape["grp"]
    assert n >= 8 and not n & (n - 1)

    def local(amounts):
        chans, length = amounts.shape
        rows = length // n
        tile = tile_of(rows)
        late = len(late_flips(n))
        relays = 2 * len(chips(n)[3])
        f32 = jnp.float32
        dma = pltpu.SemaphoreType.DMA
        regular = pltpu.SemaphoreType.REGULAR
        wide = (2 * LANES, 2 * LANES)
        table, run, weights = pl.pallas_call(
            functools.partial(exchange, n, groups),
            out_shape=[jax.ShapeDtypeStruct((n, chans, rows), f32),
                       jax.ShapeDtypeStruct((late, chans, LANES), f32),
                       jax.ShapeDtypeStruct(wide, jnp.bfloat16)],
            in_specs=[pl.BlockSpec(memory_space=pl.ANY)],
            out_specs=[pl.BlockSpec(memory_space=pltpu.VMEM)] * 3,
            scratch_shapes=[
                pltpu.VMEM((chans, length), f32),
                pltpu.VMEM((relays, chans, rows), f32),
                pltpu.VMEM((n, chans, LANES), f32),
                pltpu.VMEM((n, chans, LANES), f32),
                pltpu.VMEM((2, chans, LANES), f32),
                dma((3,)), dma, dma((2 + len(cuts_of(rows)),)), dma, dma((relays,)),
                dma, dma, dma, dma, regular, regular, regular, regular,
            ],
            compiler_params=pltpu.CompilerParams(
                collective_id=0, has_side_effects=True, vmem_limit_bytes=VMEM_GRANT),
            name="exchange",
        )(amounts)
        out = pl.pallas_call(
            functools.partial(write, n),
            out_shape=jax.ShapeDtypeStruct((n, chans, rows), f32),
            in_specs=[pl.BlockSpec(memory_space=pltpu.VMEM)] * 3,
            out_specs=pl.BlockSpec(memory_space=pl.ANY),
            scratch_shapes=[pltpu.VMEM((late, chans, tile), f32), dma],
            compiler_params=pltpu.CompilerParams(vmem_limit_bytes=VMEM_GRANT),
            name="write",
        )(table, run, weights)
        return out.reshape(n * chans, rows)

    return jax.shard_map(
        local,
        mesh=mesh,
        in_specs=(P("dev", "grp"),),
        out_specs=P(None, ("grp", "dev")),
        check_vma=False,
    )
```

time: 54.2 us -> 51.6 us (0.952)
  Pallas kernels: 54 us -> 51.5 us
    pallas_call x1, Pallas kernels: 51.9 us -> 49.5 us  [local(): pl.pallas_call(functools.partial(exchange, n, groups), out_shape=[jax.Sha...]
where the time goes in v2:
time: 51.6 us; the launch traced here: 51.5 us
  Pallas kernels  51.5 us (100%)
    pallas_call x1, Pallas kernels, local(): pl.pallas_call(functools.partial(exchange, n, groups), out_shape=[jax.Sha...  49.5 us
    pallas_call x1, Pallas kernels, local(): pl.pallas_call(functools.partial(write, n), out_shape=jax.ShapeDtypeStruc...  2.02 us

profile of v2, /device:TPU:0, one launch (start us, length us, event | category | flops | bytes accessed | tf_op | source)
XLA Modules:
  0.0 51.5 jit_solution(13823986824177743037)
XLA Ops:
  0.0 49.5 %exchange.1 = (f32[8,8,16384]{2,1,0:T(8,128)S(1)}, f32[4,8,128]{2,1,0:T(8,128)S(1)}, bf16[256,256]{1,0:T(8,128)(2,1)S(1)}) custom-call(f32[8,131072]{1,0:T(8,128)} %x_ref.1), custom_call_target="tpu_custom_call" | custom-call | tf_op jit(solution)/shard_map/exchange/pallas_call | solution.py:363
  49.5 2.0 %write.1 = f32[8,8,16384]{2,1,0:T(8,128)} custom-call(f32[8,8,16384]{2,1,0:T(8,128)S(1)} %get-tuple-element.8.t_ref, f32[4,8,128]{2,1,0:T(8,128)S(1)} %get-tuple-element.9.run_ref, bf16[256,256]{1,0:T(8,128)(2,1)S(1)} %get-tuple-element.10.w_ref), custom_call_target="tpu_custom_call" | custom-call | tf_op jit(solution)/shard_map/write/pallas_call | solution.py:383

commit v3 on v2

--- a/solution.py
+++ b/solution.py
@@ -40,7 +40,7 @@
 
 
 def cuts_of(rows):
-    cuts = [0, rows // 4, rows // 2, 3 * rows // 4, rows - tile_of(rows), rows]
+    cuts = [0, rows // 2, 3 * rows // 4, rows - tile_of(rows), rows]
     return list(zip(cuts[:-1], cuts[1:]))
 
 
@@ -69,7 +69,7 @@
 
 def exchange(n, groups, x_ref, t_ref, run_ref, w_ref, x_vm, relay_vm, give_vm, carry_vm, group_vm,
              load_sem, send_sem, recv_sem, hsend_sem, hrecv_sem, csend_sem, crecv_sem, zsend_sem, zrecv_sem,
-             note_sem, ready_sem, hello_sem, zready_sem):
+             note_sem, ready_sem, far_sem, hello_sem, zready_sem):
     me, grp = lax.axis_index("dev"), lax.axis_index("grp")
     core = lax.rem(me, 2)
     base = me - core
@@ -82,29 +82,37 @@
     late = [flip(me, k) for k in late_flips(n)]
 
     def x_core(chip):
-        return jnp.where(lax.rem(chip // 2, across // 2 + 1) > 0, 1, 0)
+        return jnp.where((chip > across) & (lax.rem(chip // 2, across // 2 + 1) == 0), 0, 1)
+
+    def y_core(chip):
+        return jnp.where((chip <= across) & (chip > 0), 0, 1)
+
+    def lead(chip):
+        return jnp.where((chip == 0) & (grp == 0), 0, 1)
 
     def targets(k):
         chip = flip(base, k)
-        first = jnp.where((chip == 0) & (grp == 0), 0, 1)
-        return [chip + first, chip + 1 - first]
+        return [chip + lead(chip), chip + 1 - lead(chip)]
 
     def signal(sem, **device):
         pl.semaphore_signal(sem, inc=1, device_id=device, device_id_type=MESH)
 
     barrier = pltpu.get_barrier_semaphore()
-    for k in ys:
-        signal(barrier, dev=flip(base, k) + 1 - x_core(base))
-    for k in xs:
-        signal(barrier, dev=flip(base, k) + x_core(flip(base, k)))
+
+    @pl.when(core == lead(base))
+    def _():
+        for k in ys:
+            signal(barrier, dev=flip(base, k) + y_core(flip(base, k)))
+        for k in xs:
+            signal(barrier, dev=flip(base, k) + x_core(flip(base, k)))
 
     @pl.when(core == 1)
     def _():
         signal(barrier, dev=base)
 
-    @pl.when((me == 0) & (grp > 0))
-    def _():
-        signal(barrier, grp=grp - 1, dev=0)
+    @pl.when((me == 1) & (grp > 0))
+    def _():
+        signal(barrier, grp=grp - 1)
 
     def at(j, lo=0, size=rows):
         return pl.ds(pl.multiple_of(j * rows + lo, LANES), size)
@@ -137,70 +145,74 @@
     def send_y(slots, spans):
         for slot in slots:
             for lo, hi in spans:
-                direct(y_blocks[slot], 1, lo, hi)
-
-    def send_d(slots, spans):
-        for slot in slots:
-            for lo, hi in spans:
-                hop(d_blocks[slot], slot, lo, hi)
-
-    turns = [(core == x_core(base), d_blocks, y_blocks, send_d, send_y),
-             (core != x_core(base), y_blocks, d_blocks, send_y, send_d)]
-
-    for mine, first, second, _, _ in turns:
-        @pl.when(mine)
+                direct(y_blocks[slot], 0, lo, hi)
+
+    def send_d():
+        for slot, j in enumerate(d_blocks):
+            hop(j, slot, 0, rows)
+
+    half = rows // 2
+    x_side, y_side = core == x_core(base), core == y_core(base)
+    openings = [(0, x_blocks[0], 0, tile), (1, y_blocks[0], 0, tile),
+                (2, x_blocks[0], tile, half), (3, y_blocks[0], tile, rows)]
+    for sem, j, lo, hi in openings:
+        load(sem, j, lo, hi - lo).start()
+    for j in [*d_blocks, *y_blocks[1:], *x_blocks[1:], me, partner]:
+        load(4, j).start()
+    load(4, x_blocks[0], half, half).start()
+
+    def await_opening(i):
+        sem, j, lo, hi = openings[i]
+        load(sem, j, lo, hi - lo).wait()
+
+    after = jnp.where((me == 1) & (grp < groups - 1), 1, 0)
+    faced = jnp.where(x_side, len(xs), 0) + jnp.where(y_side, len(ys), 0)
+    pl.semaphore_wait(barrier, faced + 1 - core + after)
+
+    for i in range(4):
+        await_opening(i)
+
+        @pl.when(y_side if i % 2 else x_side)
         def _():
-            load(0, first[0], 0, tile).start()
-            load(1, first[0], tile, rows - tile).start()
-            for j in [*first[1:], *second]:
-                load(2, j).start()
-
-    for j in [*x_blocks, me, partner]:
-        load(2, j).start()
-
-    after = jnp.where((me == 0) & (grp < groups - 1), 1, 0)
-    faced = jnp.where(core == x_core(base), 2 * len(xs), 2 * len(ys))
-    pl.semaphore_wait(barrier, faced + 1 - core + after)
-
-    for mine, first, _, send_first, _ in turns:
-        @pl.when(mine)
-        def _():
-            load(0, first[0], 0, tile).wait()
-            send_first([0], [(0, tile)])
-            load(1, first[0], tile, rows - tile).wait()
-            send_first([0], [(tile, rows)])
+            _, j, lo, hi = openings[i]
+            direct(j, 0 if i % 2 else 1, lo, hi)
 
     @pl.when(core == 0)
     def _():
         signal(note_sem, dev=base + 1)
 
-    @pl.when((me == 0) & (grp < groups - 1))
+    @pl.when((me == 1) & (grp < groups - 1))
     def _():
         signal(hello_sem, grp=grp + 1)
 
+    pl.semaphore_wait(note_sem, 1)
+
     @pl.when(core == 1)
     def _():
-        pl.semaphore_wait(note_sem, 1)
         signal(note_sem, dev=base)
+        for k in [*xs, *ys]:
+            signal(ready_sem, dev=targets(k)[0])
+
+    pl.semaphore_wait(ready_sem, jnp.where(core == lead(base), len(xs) + len(ys), 1))
+
+    @pl.when(core == lead(base))
+    def _():
+        signal(ready_sem, dev=partner)
+
+    @pl.when(core == 1)
+    def _():
         for k in xs:
-            signal(ready_sem, dev=flip(base, k))
-            signal(ready_sem, dev=flip(base, k) + 1)
-
-    load(2, 0, 0, (n - 1) * rows).wait()
-    for mine, first, _, send_first, _ in turns:
-        @pl.when(mine)
-        def _():
-            send_first(range(1, len(first)), whole)
-
-    @pl.when(core == 0)
-    def _():
-        pl.semaphore_wait(note_sem, 1)
-
-    for mine, _, second, _, send_second in turns:
-        @pl.when(mine)
-        def _():
-            send_second(range(len(second)), whole)
-
+            for j in targets(k):
+                signal(far_sem, dev=j)
+
+    load(4, 0, 0, (n - 2) * rows + half).wait()
+    send_d()
+
+    @pl.when(jnp.logical_not(y_side))
+    def _():
+        send_y([0], whole)
+
+    send_y(range(1, len(y_blocks)), whole)
     direct(partner, 0, 0, rows)
 
     shape = (2 * LANES, 2 * LANES)
@@ -223,9 +235,9 @@
 
     total = lax.fori_loop(0, n, range_total, jnp.zeros((chans, LANES), jnp.float32))
 
-    pl.semaphore_wait(ready_sem, len(xs))
-
-    @pl.when((me == 0) & (grp > 0))
+    pl.semaphore_wait(far_sem, len(xs))
+
+    @pl.when((me == 1) & (grp > 0))
     def _():
         pl.semaphore_wait(hello_sem, 1)
         signal(zready_sem, grp=grp - 1)
@@ -234,10 +246,10 @@
     def _():
         pl.semaphore_wait(zready_sem, 1)
 
-    @pl.when((me == 0) & (grp < groups - 1))
+    @pl.when((me == 1) & (grp < groups - 1))
     def _():
         for k in range(1, n):
-            signal(zready_sem, dev=k)
+            signal(zready_sem, dev=flip(me, k))
 
     def pass_on():
         return remote(group_vm.at[1], group_vm.at[0], (zsend_sem, zrecv_sem), {"grp": grp + 1})
@@ -262,9 +274,15 @@
 
     for j in [partner, *y_blocks, *x_blocks, *d_blocks]:
         remote(give_vm.at[j], carry_vm.at[me], (csend_sem, crecv_sem), {"dev": j}).start()
-    for j in x_blocks:
+
+    @pl.when(jnp.logical_not(x_side))
+    def _():
+        direct(x_blocks[0], 1, 0, half)
+
+    for slot, j in enumerate(x_blocks):
         for i, (lo, hi) in enumerate(pieces):
-            direct(j, 2 + i, lo, hi)
+            if slot or i:
+                direct(j, 1 + i, lo, hi)
 
     def scan(blocks, lo, hi, runs):
         width = min(hi - lo, 4 * tile // len(blocks))
@@ -292,13 +310,12 @@
         remote(relay_vm.at[slot], relay_vm.at[slot], (hsend_sem, hrecv_sem.at[slot]), {"dev": partner}).wait_recv()
         j = targets(ds[slot // 2] & ~across)[slot % 2]
         for i, (lo, hi) in enumerate(pieces):
-            relay(j, slot, 2 + i, lo, hi)
+            relay(j, slot, 1 + i, lo, hi)
 
     gives = carry_vm.at[pl.ds(0, n - 1)]
     remote(gives, gives, (csend_sem, crecv_sem), {"dev": partner}).wait()
-    arrived(0, 1)
+    arrived(0, 1 + len(y_blocks))
     scan([in_place(partner)], 0, rows, [carry_vm[partner]])
-    arrived(1, len(y_blocks))
     for s in range(0, len(y_blocks), 2):
         pair = y_blocks[s:s + 2]
         scan([in_place(j) for j in pair], 0, rows, [carry_vm[j] for j in pair])
@@ -306,7 +323,7 @@
     for i, j in enumerate(late):
         run_ref[i] = carry_vm[j]
     for i, (lo, hi) in enumerate(pieces[:-1]):
-        arrived(2 + i, len(late), lo, hi)
+        arrived(1 + i, len(late), lo, hi)
         for s in range(0, len(late), 4):
             four = late[s:s + 4]
             runs = scan([in_place(j) for j in four], lo, hi, [run_ref[s + r] for r in range(len(four))])
@@ -320,7 +337,7 @@
     remote(relay_vm, relay_vm, (hsend_sem, hrecv_sem.at[0]), {"dev": partner}).wait_send()
     sent = x_vm.at[:, pl.ds(0, (n - 1) * rows)]
     remote(sent, sent, (send_sem, recv_sem.at[0]), {"dev": partner}).wait_send()
-    arrived(1 + len(pieces), len(late), *pieces[-1])
+    arrived(len(pieces), len(late), *pieces[-1])
 
 
 def write(n, t_ref, run_ref, w_ref, out_ref, stage, sem):
@@ -373,8 +390,8 @@
                 pltpu.VMEM((n, chans, LANES), f32),
                 pltpu.VMEM((n, chans, LANES), f32),
                 pltpu.VMEM((2, chans, LANES), f32),
-                dma((3,)), dma, dma((2 + len(cuts_of(rows)),)), dma, dma((relays,)),
-                dma, dma, dma, dma, regular, regular, regular, regular,
+                dma((5,)), dma, dma((1 + len(cuts_of(rows)),)), dma, dma((relays,)),
+                dma, dma, dma, dma, regular, regular, regular, regular, regular,
             ],
             compiler_params=pltpu.CompilerParams(
                 collective_id=0, has_side_effects=True, vmem_limit_bytes=VMEM_GRANT),

time: 51.6 us -> 51.5 us (level); the launches traced: 51.5 us -> 50.5 us
  Pallas kernels: 51.5 us -> 50.5 us
    pallas_call x1, Pallas kernels: 49.5 us -> 48.5 us  [local(): pl.pallas_call(functools.partial(exchange, n, groups), out_shape=[jax.Sha...]
where the time goes in v3:
time: 51.5 us; the launch traced here: 50.5 us
  Pallas kernels  50.5 us (98%)
    pallas_call x1, Pallas kernels, local(): pl.pallas_call(functools.partial(exchange, n, groups), out_shape=[jax.Sha...  48.5 us
    pallas_call x1, Pallas kernels, local(): pl.pallas_call(functools.partial(write, n), out_shape=jax.ShapeDtypeStruc...  2.02 us

profile of v3, /device:TPU:0, one launch (start us, length us, event | category | flops | bytes accessed | tf_op | source)
XLA Modules:
  0.0 50.5 jit_solution(16618049994603501113)
XLA Ops:
  0.0 48.5 %exchange.1 = (f32[8,8,16384]{2,1,0:T(8,128)S(1)}, f32[4,8,128]{2,1,0:T(8,128)S(1)}, bf16[256,256]{1,0:T(8,128)(2,1)S(1)}) custom-call(f32[8,131072]{1,0:T(8,128)} %x_ref.1), custom_call_target="tpu_custom_call" | custom-call | tf_op jit(solution)/shard_map/exchange/pallas_call | solution.py:380
  48.5 2.0 %write.1 = f32[8,8,16384]{2,1,0:T(8,128)} custom-call(f32[8,8,16384]{2,1,0:T(8,128)S(1)} %get-tuple-element.8.t_ref, f32[4,8,128]{2,1,0:T(8,128)S(1)} %get-tuple-element.9.run_ref, bf16[256,256]{1,0:T(8,128)(2,1)S(1)} %get-tuple-element.10.w_ref), custom_call_target="tpu_custom_call" | custom-call | tf_op jit(solution)/shard_map/write/pallas_call | solution.py:400

commit v4 on v3

--- a/solution.py
+++ b/solution.py
@@ -77,7 +77,6 @@
     chans, rows = t_ref.shape[1:]
     tile = tile_of(rows)
     pieces = cuts_of(rows)
-    whole = [(0, rows)]
     across, xs, ys, ds = chips(n)
     late = [flip(me, k) for k in late_flips(n)]
 
@@ -117,8 +116,7 @@
     def at(j, lo=0, size=rows):
         return pl.ds(pl.multiple_of(j * rows + lo, LANES), size)
 
-    def load(sem, j, lo=0, size=rows):
-        return pltpu.make_async_copy(x_ref.at[:, at(j, lo, size)], x_vm.at[:, at(j, lo, size)], load_sem.at[sem])
+    load = pltpu.make_async_copy(x_ref, x_vm, load_sem)
 
     def remote(src, dst, sems, device):
         return pltpu.make_async_remote_copy(
@@ -126,11 +124,11 @@
             device_id=device, device_id_type=MESH)
 
     def direct(j, sem, lo, hi):
-        remote(x_vm.at[:, at(j, lo, hi - lo)], t_ref.at[me, :, pl.ds(lo, hi - lo)],
+        remote(x_ref.at[:, at(j, lo, hi - lo)], t_ref.at[me, :, pl.ds(lo, hi - lo)],
                (send_sem, recv_sem.at[sem]), {"dev": j}).start()
 
-    def hop(j, slot, lo, hi):
-        remote(x_vm.at[:, at(j, lo, hi - lo)], relay_vm.at[slot, :, pl.ds(lo, hi - lo)],
+    def hop(j, slot):
+        remote(x_ref.at[:, at(j)], relay_vm.at[slot],
                (hsend_sem, hrecv_sem.at[slot]), {"dev": flip(me, ds[slot // 2] & across)}).start()
 
     def relay(j, slot, sem, lo, hi):
@@ -142,40 +140,22 @@
     y_blocks = [j for k in ys for j in targets(k)]
     d_blocks = [j for k in ds for j in targets(k)]
 
-    def send_y(slots, spans):
-        for slot in slots:
-            for lo, hi in spans:
-                direct(y_blocks[slot], 0, lo, hi)
-
-    def send_d():
-        for slot, j in enumerate(d_blocks):
-            hop(j, slot, 0, rows)
-
     half = rows // 2
     x_side, y_side = core == x_core(base), core == y_core(base)
-    openings = [(0, x_blocks[0], 0, tile), (1, y_blocks[0], 0, tile),
-                (2, x_blocks[0], tile, half), (3, y_blocks[0], tile, rows)]
-    for sem, j, lo, hi in openings:
-        load(sem, j, lo, hi - lo).start()
-    for j in [*d_blocks, *y_blocks[1:], *x_blocks[1:], me, partner]:
-        load(4, j).start()
-    load(4, x_blocks[0], half, half).start()
-
-    def await_opening(i):
-        sem, j, lo, hi = openings[i]
-        load(sem, j, lo, hi - lo).wait()
 
     after = jnp.where((me == 1) & (grp < groups - 1), 1, 0)
     faced = jnp.where(x_side, len(xs), 0) + jnp.where(y_side, len(ys), 0)
     pl.semaphore_wait(barrier, faced + 1 - core + after)
 
-    for i in range(4):
-        await_opening(i)
-
-        @pl.when(y_side if i % 2 else x_side)
-        def _():
-            _, j, lo, hi = openings[i]
-            direct(j, 0 if i % 2 else 1, lo, hi)
+    @pl.when(x_side)
+    def _():
+        direct(x_blocks[0], 1, 0, half)
+
+    @pl.when(y_side)
+    def _():
+        direct(y_blocks[0], 0, 0, rows)
+
+    load.start()
 
     @pl.when(core == 0)
     def _():
@@ -205,15 +185,16 @@
             for j in targets(k):
                 signal(far_sem, dev=j)
 
-    load(4, 0, 0, (n - 2) * rows + half).wait()
-    send_d()
+    for slot, j in enumerate(d_blocks):
+        hop(j, slot)
 
     @pl.when(jnp.logical_not(y_side))
     def _():
-        send_y([0], whole)
-
-    send_y(range(1, len(y_blocks)), whole)
-    direct(partner, 0, 0, rows)
+        direct(y_blocks[0], 0, 0, rows)
+
+    for j in [*y_blocks[1:], partner]:
+        direct(j, 0, 0, rows)
+    load.wait()
 
     shape = (2 * LANES, 2 * LANES)
     row = lax.rem(lax.broadcasted_iota(jnp.int32, shape, 0), LANES)
@@ -390,7 +371,7 @@
                 pltpu.VMEM((n, chans, LANES), f32),
                 pltpu.VMEM((n, chans, LANES), f32),
                 pltpu.VMEM((2, chans, LANES), f32),
-                dma((5,)), dma, dma((1 + len(cuts_of(rows)),)), dma, dma((relays,)),
+                dma, dma, dma((1 + len(cuts_of(rows)),)), dma, dma((relays,)),
                 dma, dma, dma, dma, regular, regular, regular, regular, regular,
             ],
             compiler_params=pltpu.CompilerParams(

time: 51.5 us -> 51 us (level); the launches traced: 50.5 us -> 50.8 us
  no operation moved by 1% of the time
where the time goes in v4:
time: 51 us; the launch traced here: 50.8 us
  Pallas kernels  50.8 us (100%)
    pallas_call x1, Pallas kernels, local(): pl.pallas_call(functools.partial(exchange, n, groups), out_shape=[jax.Sha...  48.8 us
    pallas_call x1, Pallas kernels, local(): pl.pallas_call(functools.partial(write, n), out_shape=jax.ShapeDtypeStruc...  2.02 us

profile of v4, /device:TPU:0, one launch (start us, length us, event | category | flops | bytes accessed | tf_op | source)
XLA Modules:
  0.0 50.8 jit_solution(9643910439964323212)
XLA Ops:
  0.0 48.8 %exchange.1 = (f32[8,8,16384]{2,1,0:T(8,128)S(1)}, f32[4,8,128]{2,1,0:T(8,128)S(1)}, bf16[256,256]{1,0:T(8,128)(2,1)S(1)}) custom-call(f32[8,131072]{1,0:T(8,128)} %x_ref.1), custom_call_target="tpu_custom_call" | custom-call | tf_op jit(solution)/shard_map/exchange/pallas_call | solution.py:361
  48.8 2.0 %write.1 = f32[8,8,16384]{2,1,0:T(8,128)} custom-call(f32[8,8,16384]{2,1,0:T(8,128)S(1)} %get-tuple-element.8.t_ref, f32[4,8,128]{2,1,0:T(8,128)S(1)} %get-tuple-element.9.run_ref, bf16[256,256]{1,0:T(8,128)(2,1)S(1)} %get-tuple-element.10.w_ref), custom_call_target="tpu_custom_call" | custom-call | tf_op jit(solution)/shard_map/write/pallas_call | solution.py:381

commit v5 on v4

--- a/solution.py
+++ b/solution.py
@@ -91,7 +91,11 @@
 
     def targets(k):
         chip = flip(base, k)
-        return [chip + lead(chip), chip + 1 - lead(chip)]
+        first = jnp.where((chip == 0) & (grp == 0), 0, core)
+        return [chip + first, chip + 1 - first]
+
+    def front(k):
+        return flip(base, k) + lead(flip(base, k))
 
     def signal(sem, **device):
         pl.semaphore_signal(sem, inc=1, device_id=device, device_id_type=MESH)
@@ -140,7 +144,7 @@
     y_blocks = [j for k in ys for j in targets(k)]
     d_blocks = [j for k in ds for j in targets(k)]
 
-    half = rows // 2
+    head = 3 * rows // 8
     x_side, y_side = core == x_core(base), core == y_core(base)
 
     after = jnp.where((me == 1) & (grp < groups - 1), 1, 0)
@@ -149,11 +153,11 @@
 
     @pl.when(x_side)
     def _():
-        direct(x_blocks[0], 1, 0, half)
+        direct(front(xs[0]), 1, 0, head)
 
     @pl.when(y_side)
     def _():
-        direct(y_blocks[0], 0, 0, rows)
+        direct(front(ys[0]), 0, 0, head)
 
     load.start()
 
@@ -166,12 +170,28 @@
         signal(hello_sem, grp=grp + 1)
 
     pl.semaphore_wait(note_sem, 1)
+
+    @pl.when(jnp.logical_not(x_side))
+    def _():
+        direct(front(xs[0]), 1, 0, head)
+
+    @pl.when(jnp.logical_not(y_side))
+    def _():
+        direct(front(ys[0]), 0, 0, head)
+
+    def unopened(slot, opened, j, sem):
+        if slot > 1:
+            direct(j, sem, 0, head)
+        else:
+            @pl.when(j != opened)
+            def _():
+                direct(j, sem, 0, head)
 
     @pl.when(core == 1)
     def _():
         signal(note_sem, dev=base)
         for k in [*xs, *ys]:
-            signal(ready_sem, dev=targets(k)[0])
+            signal(ready_sem, dev=front(k))
 
     pl.semaphore_wait(ready_sem, jnp.where(core == lead(base), len(xs) + len(ys), 1))
 
@@ -187,13 +207,10 @@
 
     for slot, j in enumerate(d_blocks):
         hop(j, slot)
-
-    @pl.when(jnp.logical_not(y_side))
-    def _():
-        direct(y_blocks[0], 0, 0, rows)
-
-    for j in [*y_blocks[1:], partner]:
-        direct(j, 0, 0, rows)
+    for slot, j in enumerate(y_blocks):
+        unopened(slot, front(ys[0]), j, 0)
+        direct(j, 0, head, rows)
+    direct(partner, 0, 0, rows)
     load.wait()
 
     shape = (2 * LANES, 2 * LANES)
@@ -255,15 +272,6 @@
 
     for j in [partner, *y_blocks, *x_blocks, *d_blocks]:
         remote(give_vm.at[j], carry_vm.at[me], (csend_sem, crecv_sem), {"dev": j}).start()
-
-    @pl.when(jnp.logical_not(x_side))
-    def _():
-        direct(x_blocks[0], 1, 0, half)
-
-    for slot, j in enumerate(x_blocks):
-        for i, (lo, hi) in enumerate(pieces):
-            if slot or i:
-                direct(j, 1 + i, lo, hi)
 
     def scan(blocks, lo, hi, runs):
         width = min(hi - lo, 4 * tile // len(blocks))
@@ -287,6 +295,11 @@
         remote(span, span, (send_sem, recv_sem.at[sem]), {"dev": partner}).wait_recv()
 
     scan([(x_vm, me * rows, t_ref.at[me])], 0, rows, [carry_vm[me]])
+    for slot, j in enumerate(x_blocks):
+        unopened(slot, front(xs[0]), j, 1)
+        for i, (lo, hi) in enumerate(pieces):
+            direct(j, 1 + i, lo if i else head, hi)
+
     for slot in range(len(d_blocks)):
         remote(relay_vm.at[slot], relay_vm.at[slot], (hsend_sem, hrecv_sem.at[slot]), {"dev": partner}).wait_recv()
         j = targets(ds[slot // 2] & ~across)[slot % 2]

time: 51 us -> 51 us (level)
  no operation moved by 1% of the time
where the time goes in v5:
time: 51 us; the launch traced here: 50.8 us
  Pallas kernels  50.8 us (100%)
    pallas_call x1, Pallas kernels, local(): pl.pallas_call(functools.partial(exchange, n, groups), out_shape=[jax.Sha...  48.8 us
    pallas_call x1, Pallas kernels, local(): pl.pallas_call(functools.partial(write, n), out_shape=jax.ShapeDtypeStruc...  2.02 us

profile of v5, /device:TPU:0, one launch (start us, length us, event | category | flops | bytes accessed | tf_op | source)
XLA Modules:
  0.0 50.8 jit_solution(16331752267755574221)
XLA Ops:
  0.0 48.8 %exchange.1 = (f32[8,8,16384]{2,1,0:T(8,128)S(1)}, f32[4,8,128]{2,1,0:T(8,128)S(1)}, bf16[256,256]{1,0:T(8,128)(2,1)S(1)}) custom-call(f32[8,131072]{1,0:T(8,128)} %x_ref.1), custom_call_target="tpu_custom_call" | custom-call | tf_op jit(solution)/shard_map/exchange/pallas_call | solution.py:374
  48.8 2.0 %write.1 = f32[8,8,16384]{2,1,0:T(8,128)} custom-call(f32[8,8,16384]{2,1,0:T(8,128)S(1)} %get-tuple-element.8.t_ref, f32[4,8,128]{2,1,0:T(8,128)S(1)} %get-tuple-element.9.run_ref, bf16[256,256]{1,0:T(8,128)(2,1)S(1)} %get-tuple-element.10.w_ref), custom_call_target="tpu_custom_call" | custom-call | tf_op jit(solution)/shard_map/write/pallas_call | solution.py:394

commit v6 on v4

--- a/solution.py
+++ b/solution.py
@@ -67,6 +67,10 @@
     return outs, after
 
 
+def last_lane(tile):
+    return jnp.broadcast_to(tile[:, LANES - 1:], tile.shape)
+
+
 def exchange(n, groups, x_ref, t_ref, run_ref, w_ref, x_vm, relay_vm, give_vm, carry_vm, group_vm,
              load_sem, send_sem, recv_sem, hsend_sem, hrecv_sem, csend_sem, crecv_sem, zsend_sem, zrecv_sem,
              note_sem, ready_sem, far_sem, hello_sem, zready_sem):
@@ -123,13 +127,14 @@
             src_ref=src, dst_ref=dst, send_sem=sems[0], recv_sem=sems[1],
             device_id=device, device_id_type=MESH)
 
-    def direct(j, sem, lo, hi):
-        remote(x_ref.at[:, at(j, lo, hi - lo)], t_ref.at[me, :, pl.ds(lo, hi - lo)],
+    def direct(j, sem, lo, hi, source=x_ref):
+        remote(source.at[:, at(j, lo, hi - lo)], t_ref.at[me, :, pl.ds(lo, hi - lo)],
                (send_sem, recv_sem.at[sem]), {"dev": j}).start()
 
-    def hop(j, slot):
-        remote(x_ref.at[:, at(j)], relay_vm.at[slot],
-               (hsend_sem, hrecv_sem.at[slot]), {"dev": flip(me, ds[slot // 2] & across)}).start()
+    def hop(j, slot, part, source):
+        lo, hi = parts[part]
+        remote(source.at[:, at(j, lo, hi - lo)], relay_vm.at[slot, :, pl.ds(lo, hi - lo)],
+               (hsend_sem, hrecv_sem.at[slot, part]), {"dev": flip(me, ds[slot // 2] & across)}).start()
 
     def relay(j, slot, sem, lo, hi):
         source = flip(me, ds[slot // 2] & across)
@@ -141,6 +146,8 @@
     d_blocks = [j for k in ds for j in targets(k)]
 
     half = rows // 2
+    main = rows - tile
+    parts = [(0, main), (main, rows)]
     x_side, y_side = core == x_core(base), core == y_core(base)
 
     after = jnp.where((me == 1) & (grp < groups - 1), 1, 0)
@@ -153,7 +160,7 @@
 
     @pl.when(y_side)
     def _():
-        direct(y_blocks[0], 0, 0, rows)
+        direct(y_blocks[0], 0, 0, main)
 
     load.start()
 
@@ -186,14 +193,15 @@
                 signal(far_sem, dev=j)
 
     for slot, j in enumerate(d_blocks):
-        hop(j, slot)
+        hop(j, slot, 0, x_ref)
 
     @pl.when(jnp.logical_not(y_side))
     def _():
-        direct(y_blocks[0], 0, 0, rows)
-
-    for j in [*y_blocks[1:], partner]:
-        direct(j, 0, 0, rows)
+        direct(y_blocks[0], 0, 0, main)
+
+    for j in y_blocks[1:]:
+        direct(j, 0, 0, main)
+    direct(partner, 0, 0, rows)
     load.wait()
 
     shape = (2 * LANES, 2 * LANES)
@@ -253,8 +261,16 @@
     def _():
         pass_on().start()
 
-    for j in [partner, *y_blocks, *x_blocks, *d_blocks]:
-        remote(give_vm.at[j], carry_vm.at[me], (csend_sem, crecv_sem), {"dev": j}).start()
+    lane = lax.broadcasted_iota(jnp.int32, (chans, LANES), 1)
+    for j in range(n):
+        end = pl.ds((j + 1) * rows - LANES, LANES)
+        x_vm[:, end] = jnp.where(lane == LANES - 1, give_vm[j], x_vm[:, end])
+    given = remote(give_vm.at[partner], carry_vm.at[me], (csend_sem, crecv_sem), {"dev": partner})
+    given.start()
+    for slot, j in enumerate(d_blocks):
+        hop(j, slot, 1, x_vm)
+    for j in y_blocks:
+        direct(j, 0, main, rows, x_vm)
 
     @pl.when(jnp.logical_not(x_side))
     def _():
@@ -263,7 +279,7 @@
     for slot, j in enumerate(x_blocks):
         for i, (lo, hi) in enumerate(pieces):
             if slot or i:
-                direct(j, 1 + i, lo, hi)
+                direct(j, 1 + i, lo, hi, x_vm if hi == rows else x_ref)
 
     def scan(blocks, lo, hi, runs):
         width = min(hi - lo, 4 * tile // len(blocks))
@@ -287,22 +303,30 @@
         remote(span, span, (send_sem, recv_sem.at[sem]), {"dev": partner}).wait_recv()
 
     scan([(x_vm, me * rows, t_ref.at[me])], 0, rows, [carry_vm[me]])
+    def forward(slot, part):
+        lo, hi = parts[part]
+        span = relay_vm.at[slot, :, pl.ds(lo, hi - lo)]
+        remote(span, span, (hsend_sem, hrecv_sem.at[slot, part]), {"dev": partner}).wait_recv()
+        j = targets(ds[slot // 2] & ~across)[slot % 2]
+        for i, (start, end) in enumerate(pieces):
+            if lo <= start < hi:
+                relay(j, slot, 1 + i, start, end)
+
     for slot in range(len(d_blocks)):
-        remote(relay_vm.at[slot], relay_vm.at[slot], (hsend_sem, hrecv_sem.at[slot]), {"dev": partner}).wait_recv()
-        j = targets(ds[slot // 2] & ~across)[slot % 2]
-        for i, (lo, hi) in enumerate(pieces):
-            relay(j, slot, 1 + i, lo, hi)
-
-    gives = carry_vm.at[pl.ds(0, n - 1)]
-    remote(gives, gives, (csend_sem, crecv_sem), {"dev": partner}).wait()
+        forward(slot, 0)
+    for slot in range(len(d_blocks)):
+        forward(slot, 1)
+
+    given.wait()
     arrived(0, 1 + len(y_blocks))
     scan([in_place(partner)], 0, rows, [carry_vm[partner]])
     for s in range(0, len(y_blocks), 2):
         pair = y_blocks[s:s + 2]
-        scan([in_place(j) for j in pair], 0, rows, [carry_vm[j] for j in pair])
-
-    for i, j in enumerate(late):
-        run_ref[i] = carry_vm[j]
+        runs = [last_lane(t_ref[j, :, pl.ds(rows - LANES, LANES)]) for j in pair]
+        scan([in_place(j) for j in pair], 0, rows, runs)
+
+    for i in range(len(late)):
+        run_ref[i] = jnp.zeros((chans, LANES), jnp.float32)
     for i, (lo, hi) in enumerate(pieces[:-1]):
         arrived(1 + i, len(late), lo, hi)
         for s in range(0, len(late), 4):
@@ -315,7 +339,7 @@
     def _():
         pass_on().wait_send()
 
-    remote(relay_vm, relay_vm, (hsend_sem, hrecv_sem.at[0]), {"dev": partner}).wait_send()
+    remote(relay_vm, relay_vm, (hsend_sem, hrecv_sem.at[0, 0]), {"dev": partner}).wait_send()
     sent = x_vm.at[:, pl.ds(0, (n - 1) * rows)]
     remote(sent, sent, (send_sem, recv_sem.at[0]), {"dev": partner}).wait_send()
     arrived(len(pieces), len(late), *pieces[-1])
@@ -326,21 +350,29 @@
     rows = t_ref.shape[2]
     tile = tile_of(rows)
     late = late_flips(n)
-    main, last = pl.ds(0, rows - tile), pl.ds(rows - tile, tile)
+    last = pl.ds(rows - tile, tile)
 
     for k in range(n):
-        j = flip(me, k)
-        if k in late:
-            pltpu.make_async_copy(t_ref.at[j, :, main], out_ref.at[j, :, main], sem).start()
-        else:
+        if k not in late:
+            j = flip(me, k)
             pltpu.make_async_copy(t_ref.at[j], out_ref.at[j], sem).start()
     for s in range(0, len(late), 4):
-        four = late[s:s + 4]
-        outs, _ = scan_tiles([t_ref[flip(me, k), :, last] for k in four], w_ref, [run_ref[s + r] for r in range(len(four))])
-        for r, (k, parts) in enumerate(zip(four, outs)):
-            for j, sums in enumerate(parts):
-                stage[s + r, :, pl.ds(j * LANES, LANES)] = sums
-            pltpu.make_async_copy(stage.at[s + r], out_ref.at[flip(me, k), :, last], sem).start()
+        four = [flip(me, k) for k in late[s:s + 4]]
+        carries = [last_lane(t_ref[j, :, pl.ds(rows - LANES, LANES)]) for j in four]
+        runs = [run_ref[s + r] + carry for r, carry in enumerate(carries)]
+        outs, _ = scan_tiles([t_ref[j, :, last] for j in four], w_ref, runs)
+        for r, (j, carry, parts) in enumerate(zip(four, carries, outs)):
+            wide = jnp.concatenate([carry] * (tile // LANES), axis=1)
+
+            def add(i, _):
+                at = pl.ds(pl.multiple_of(i * tile, LANES), tile)
+                stage[s + r, :, at] = t_ref[j, :, at] + wide
+                return 0
+
+            lax.fori_loop(0, rows // tile - 1, add, 0, unroll=True)
+            for i, sums in enumerate(parts):
+                stage[s + r, :, pl.ds(rows - tile + i * LANES, LANES)] = sums
+            pltpu.make_async_copy(stage.at[s + r], out_ref.at[j], sem).start()
     pltpu.make_async_copy(t_ref, out_ref, sem).wait()
 
 
@@ -351,7 +383,6 @@
     def local(amounts):
         chans, length = amounts.shape
         rows = length // n
-        tile = tile_of(rows)
         late = len(late_flips(n))
         relays = 2 * len(chips(n)[3])
         f32 = jnp.float32
@@ -371,7 +402,7 @@
                 pltpu.VMEM((n, chans, LANES), f32),
                 pltpu.VMEM((n, chans, LANES), f32),
                 pltpu.VMEM((2, chans, LANES), f32),
-                dma, dma, dma((1 + len(cuts_of(rows)),)), dma, dma((relays,)),
+                dma, dma, dma((1 + len(cuts_of(rows)),)), dma, dma((relays, 2)),
                 dma, dma, dma, dma, regular, regular, regular, regular, regular,
             ],
             compiler_params=pltpu.CompilerParams(
@@ -383,7 +414,7 @@
             out_shape=jax.ShapeDtypeStruct((n, chans, rows), f32),
             in_specs=[pl.BlockSpec(memory_space=pltpu.VMEM)] * 3,
             out_specs=pl.BlockSpec(memory_space=pl.ANY),
-            scratch_shapes=[pltpu.VMEM((late, chans, tile), f32), dma],
+            scratch_shapes=[pltpu.VMEM((late, chans, rows), f32), dma],
             compiler_params=pltpu.CompilerParams(vmem_limit_bytes=VMEM_GRANT),
             name="write",
         )(table, run, weights)

time: 51 us -> 50.5 us (level)
  no operation moved by 1% of the time
where the time goes in v6:
time: 50.5 us; the launch traced here: 50.4 us
  Pallas kernels  50.4 us (100%)
    pallas_call x1, Pallas kernels, local(): pl.pallas_call(functools.partial(exchange, n, groups), out_shape=[jax.Sha...  48.3 us
    pallas_call x1, Pallas kernels, local(): pl.pallas_call(functools.partial(write, n), out_shape=jax.ShapeDtypeStruc...  2.04 us

profile of v6, /device:TPU:0, one launch (start us, length us, event | category | flops | bytes accessed | tf_op | source)
XLA Modules:
  0.0 50.4 jit_solution(15532727979196211914)
XLA Ops:
  0.0 48.3 %exchange.1 = (f32[8,8,16384]{2,1,0:T(8,128)S(1)}, f32[4,8,128]{2,1,0:T(8,128)S(1)}, bf16[256,256]{1,0:T(8,128)(2,1)S(1)}) custom-call(f32[8,131072]{1,0:T(8,128)} %x_ref.1), custom_call_target="tpu_custom_call" | custom-call | tf_op jit(solution)/shard_map/exchange/pallas_call | solution.py:392
  48.4 2.0 %write.1 = f32[8,8,16384]{2,1,0:T(8,128)} custom-call(f32[8,8,16384]{2,1,0:T(8,128)S(1)} %get-tuple-element.8.t_ref, f32[4,8,128]{2,1,0:T(8,128)S(1)} %get-tuple-element.9.run_ref, bf16[256,256]{1,0:T(8,128)(2,1)S(1)} %get-tuple-element.10.w_ref), custom_call_target="tpu_custom_call" | custom-call | tf_op jit(solution)/shard_map/write/pallas_call | solution.py:412

commit v7 on v6

--- a/solution.py
+++ b/solution.py
@@ -71,8 +71,8 @@
     return jnp.broadcast_to(tile[:, LANES - 1:], tile.shape)
 
 
-def exchange(n, groups, x_ref, t_ref, run_ref, w_ref, x_vm, relay_vm, give_vm, carry_vm, group_vm,
-             load_sem, send_sem, recv_sem, hsend_sem, hrecv_sem, csend_sem, crecv_sem, zsend_sem, zrecv_sem,
+def exchange(n, groups, x_ref, t_ref, run_ref, w_ref, x_vm, relay_vm, give_vm, group_vm,
+             load_sem, send_sem, recv_sem, hsend_sem, hrecv_sem, zsend_sem, zrecv_sem,
              note_sem, ready_sem, far_sem, hello_sem, zready_sem):
     me, grp = lax.axis_index("dev"), lax.axis_index("grp")
     core = lax.rem(me, 2)
@@ -134,7 +134,7 @@
     def hop(j, slot, part, source):
         lo, hi = parts[part]
         remote(source.at[:, at(j, lo, hi - lo)], relay_vm.at[slot, :, pl.ds(lo, hi - lo)],
-               (hsend_sem, hrecv_sem.at[slot, part]), {"dev": flip(me, ds[slot // 2] & across)}).start()
+               (hsend_sem, hrecv_sem.at[len(d_blocks) if part else slot]), {"dev": flip(me, ds[slot // 2] & across)}).start()
 
     def relay(j, slot, sem, lo, hi):
         source = flip(me, ds[slot // 2] & across)
@@ -201,7 +201,7 @@
 
     for j in y_blocks[1:]:
         direct(j, 0, 0, main)
-    direct(partner, 0, 0, rows)
+    direct(partner, 0, 0, main)
     load.wait()
 
     shape = (2 * LANES, 2 * LANES)
@@ -255,7 +255,6 @@
     group_vm[1] = before + total
     for j in range(n):
         give_vm[j] = give_vm[j] + before
-    carry_vm[me] = give_vm[me]
 
     @pl.when(grp < groups - 1)
     def _():
@@ -265,8 +264,7 @@
     for j in range(n):
         end = pl.ds((j + 1) * rows - LANES, LANES)
         x_vm[:, end] = jnp.where(lane == LANES - 1, give_vm[j], x_vm[:, end])
-    given = remote(give_vm.at[partner], carry_vm.at[me], (csend_sem, crecv_sem), {"dev": partner})
-    given.start()
+    direct(partner, 0, main, rows, x_vm)
     for slot, j in enumerate(d_blocks):
         hop(j, slot, 1, x_vm)
     for j in y_blocks:
@@ -302,24 +300,24 @@
         span = t_ref.at[pl.ds(0, blocks), :, pl.ds(lo, hi - lo)]
         remote(span, span, (send_sem, recv_sem.at[sem]), {"dev": partner}).wait_recv()
 
-    scan([(x_vm, me * rows, t_ref.at[me])], 0, rows, [carry_vm[me]])
-    def forward(slot, part):
+    scan([(x_vm, me * rows, t_ref.at[me])], 0, rows, [give_vm[me]])
+    def forward(slots, part):
         lo, hi = parts[part]
-        span = relay_vm.at[slot, :, pl.ds(lo, hi - lo)]
-        remote(span, span, (hsend_sem, hrecv_sem.at[slot, part]), {"dev": partner}).wait_recv()
-        j = targets(ds[slot // 2] & ~across)[slot % 2]
-        for i, (start, end) in enumerate(pieces):
-            if lo <= start < hi:
-                relay(j, slot, 1 + i, start, end)
+        span = relay_vm.at[pl.ds(slots[0], len(slots)), :, pl.ds(lo, hi - lo)]
+        sem = hrecv_sem.at[len(d_blocks) if part else slots[0]]
+        remote(span, span, (hsend_sem, sem), {"dev": partner}).wait_recv()
+        for slot in slots:
+            j = targets(ds[slot // 2] & ~across)[slot % 2]
+            for i, (start, end) in enumerate(pieces):
+                if lo <= start < hi:
+                    relay(j, slot, 1 + i, start, end)
 
     for slot in range(len(d_blocks)):
-        forward(slot, 0)
-    for slot in range(len(d_blocks)):
-        forward(slot, 1)
-
-    given.wait()
+        forward([slot], 0)
+    forward(range(len(d_blocks)), 1)
+
     arrived(0, 1 + len(y_blocks))
-    scan([in_place(partner)], 0, rows, [carry_vm[partner]])
+    scan([in_place(partner)], 0, rows, [last_lane(t_ref[partner, :, pl.ds(rows - LANES, LANES)])])
     for s in range(0, len(y_blocks), 2):
         pair = y_blocks[s:s + 2]
         runs = [last_lane(t_ref[j, :, pl.ds(rows - LANES, LANES)]) for j in pair]
@@ -339,7 +337,7 @@
     def _():
         pass_on().wait_send()
 
-    remote(relay_vm, relay_vm, (hsend_sem, hrecv_sem.at[0, 0]), {"dev": partner}).wait_send()
+    remote(relay_vm, relay_vm, (hsend_sem, hrecv_sem.at[0]), {"dev": partner}).wait_send()
     sent = x_vm.at[:, pl.ds(0, (n - 1) * rows)]
     remote(sent, sent, (send_sem, recv_sem.at[0]), {"dev": partner}).wait_send()
     arrived(len(pieces), len(late), *pieces[-1])
@@ -400,10 +398,9 @@
                 pltpu.VMEM((chans, length), f32),
                 pltpu.VMEM((relays, chans, rows), f32),
                 pltpu.VMEM((n, chans, LANES), f32),
-                pltpu.VMEM((n, chans, LANES), f32),
                 pltpu.VMEM((2, chans, LANES), f32),
-                dma, dma, dma((1 + len(cuts_of(rows)),)), dma, dma((relays, 2)),
-                dma, dma, dma, dma, regular, regular, regular, regular, regular,
+                dma, dma, dma((1 + len(cuts_of(rows)),)), dma, dma((relays + 1,)),
+                dma, dma, regular, regular, regular, regular, regular,
             ],
             compiler_params=pltpu.CompilerParams(
                 collective_id=0, has_side_effects=True, vmem_limit_bytes=VMEM_GRANT),

time: 50.5 us -> 50.5 us (level)
  no operation moved by 1% of the time
where the time goes in v7:
time: 50.5 us; the launch traced here: 50.4 us
  Pallas kernels  50.4 us (100%)
    pallas_call x1, Pallas kernels, local(): pl.pallas_call(functools.partial(exchange, n, groups), out_shape=[jax.Sha...  48.3 us
    pallas_call x1, Pallas kernels, local(): pl.pallas_call(functools.partial(write, n), out_shape=jax.ShapeDtypeStruc...  2.04 us

profile of v7, /device:TPU:0, one launch (start us, length us, event | category | flops | bytes accessed | tf_op | source)
XLA Modules:
  0.0 50.4 jit_solution(10462349461432568936)
XLA Ops:
  0.0 48.3 %exchange.1 = (f32[8,8,16384]{2,1,0:T(8,128)S(1)}, f32[4,8,128]{2,1,0:T(8,128)S(1)}, bf16[256,256]{1,0:T(8,128)(2,1)S(1)}) custom-call(f32[8,131072]{1,0:T(8,128)} %x_ref.1), custom_call_target="tpu_custom_call" | custom-call | tf_op jit(solution)/shard_map/exchange/pallas_call | solution.py:390
  48.3 2.0 %write.1 = f32[8,8,16384]{2,1,0:T(8,128)} custom-call(f32[8,8,16384]{2,1,0:T(8,128)S(1)} %get-tuple-element.8.t_ref, f32[4,8,128]{2,1,0:T(8,128)S(1)} %get-tuple-element.9.run_ref, bf16[256,256]{1,0:T(8,128)(2,1)S(1)} %get-tuple-element.10.w_ref), custom_call_target="tpu_custom_call" | custom-call | tf_op jit(solution)/shard_map/write/pallas_call | solution.py:409

commit v8 on v6

--- a/solution.py
+++ b/solution.py
@@ -115,7 +115,7 @@
 
     @pl.when((me == 1) & (grp > 0))
     def _():
-        signal(barrier, grp=grp - 1)
+        signal(barrier, grp=grp - 1, dev=0)
 
     def at(j, lo=0, size=rows):
         return pl.ds(pl.multiple_of(j * rows + lo, LANES), size)
@@ -150,7 +150,7 @@
     parts = [(0, main), (main, rows)]
     x_side, y_side = core == x_core(base), core == y_core(base)
 
-    after = jnp.where((me == 1) & (grp < groups - 1), 1, 0)
+    after = jnp.where((me == 0) & (grp < groups - 1), 1, 0)
     faced = jnp.where(x_side, len(xs), 0) + jnp.where(y_side, len(ys), 0)
     pl.semaphore_wait(barrier, faced + 1 - core + after)
 
@@ -168,11 +168,11 @@
     def _():
         signal(note_sem, dev=base + 1)
 
+    pl.semaphore_wait(note_sem, 1)
+
     @pl.when((me == 1) & (grp < groups - 1))
     def _():
         signal(hello_sem, grp=grp + 1)
-
-    pl.semaphore_wait(note_sem, 1)
 
     @pl.when(core == 1)
     def _():

time: 50.5 us -> 50.5 us (level)
  no operation moved by 1% of the time
where the time goes in v8:
time: 50.5 us; the launch traced here: 50.4 us
  Pallas kernels  50.4 us (100%)
    pallas_call x1, Pallas kernels, local(): pl.pallas_call(functools.partial(exchange, n, groups), out_shape=[jax.Sha...  48.3 us
    pallas_call x1, Pallas kernels, local(): pl.pallas_call(functools.partial(write, n), out_shape=jax.ShapeDtypeStruc...  2.04 us

profile of v8, /device:TPU:0, one launch (start us, length us, event | category | flops | bytes accessed | tf_op | source)
XLA Modules:
  0.0 50.4 jit_solution(8259024875193368849)
XLA Ops:
  0.0 48.3 %exchange.1 = (f32[8,8,16384]{2,1,0:T(8,128)S(1)}, f32[4,8,128]{2,1,0:T(8,128)S(1)}, bf16[256,256]{1,0:T(8,128)(2,1)S(1)}) custom-call(f32[8,131072]{1,0:T(8,128)} %x_ref.1), custom_call_target="tpu_custom_call" | custom-call | tf_op jit(solution)/shard_map/exchange/pallas_call | solution.py:392
  48.3 2.0 %write.1 = f32[8,8,16384]{2,1,0:T(8,128)} custom-call(f32[8,8,16384]{2,1,0:T(8,128)S(1)} %get-tuple-element.8.t_ref, f32[4,8,128]{2,1,0:T(8,128)S(1)} %get-tuple-element.9.run_ref, bf16[256,256]{1,0:T(8,128)(2,1)S(1)} %get-tuple-element.10.w_ref), custom_call_target="tpu_custom_call" | custom-call | tf_op jit(solution)/shard_map/write/pallas_call | solution.py:412

commit v9 on v7

--- a/solution.py
+++ b/solution.py
@@ -115,7 +115,7 @@
 
     @pl.when((me == 1) & (grp > 0))
     def _():
-        signal(barrier, grp=grp - 1)
+        signal(barrier, grp=grp - 1, dev=0)
 
     def at(j, lo=0, size=rows):
         return pl.ds(pl.multiple_of(j * rows + lo, LANES), size)
@@ -150,7 +150,7 @@
     parts = [(0, main), (main, rows)]
     x_side, y_side = core == x_core(base), core == y_core(base)
 
-    after = jnp.where((me == 1) & (grp < groups - 1), 1, 0)
+    after = jnp.where((me == 0) & (grp < groups - 1), 1, 0)
     faced = jnp.where(x_side, len(xs), 0) + jnp.where(y_side, len(ys), 0)
     pl.semaphore_wait(barrier, faced + 1 - core + after)
 
@@ -168,11 +168,11 @@
     def _():
         signal(note_sem, dev=base + 1)
 
+    pl.semaphore_wait(note_sem, 1)
+
     @pl.when((me == 1) & (grp < groups - 1))
     def _():
         signal(hello_sem, grp=grp + 1)
-
-    pl.semaphore_wait(note_sem, 1)
 
     @pl.when(core == 1)
     def _():

time: 50.5 us -> 50.5 us (level)
  no operation moved by 1% of the time
where the time goes in v9:
time: 50.5 us; the launch traced here: 50.3 us
  Pallas kernels  50.3 us (100%)
    pallas_call x1, Pallas kernels, local(): pl.pallas_call(functools.partial(exchange, n, groups), out_shape=[jax.Sha...  48.3 us
    pallas_call x1, Pallas kernels, local(): pl.pallas_call(functools.partial(write, n), out_shape=jax.ShapeDtypeStruc...  2.04 us

profile of v9, /device:TPU:0, one launch (start us, length us, event | category | flops | bytes accessed | tf_op | source)
XLA Modules:
  0.0 50.3 jit_solution(14176933917909489183)
XLA Ops:
  0.0 48.3 %exchange.1 = (f32[8,8,16384]{2,1,0:T(8,128)S(1)}, f32[4,8,128]{2,1,0:T(8,128)S(1)}, bf16[256,256]{1,0:T(8,128)(2,1)S(1)}) custom-call(f32[8,131072]{1,0:T(8,128)} %x_ref.1), custom_call_target="tpu_custom_call" | custom-call | tf_op jit(solution)/shard_map/exchange/pallas_call | solution.py:390
  48.3 2.0 %write.1 = f32[8,8,16384]{2,1,0:T(8,128)} custom-call(f32[8,8,16384]{2,1,0:T(8,128)S(1)} %get-tuple-element.8.t_ref, f32[4,8,128]{2,1,0:T(8,128)S(1)} %get-tuple-element.9.run_ref, bf16[256,256]{1,0:T(8,128)(2,1)S(1)} %get-tuple-element.10.w_ref), custom_call_target="tpu_custom_call" | custom-call | tf_op jit(solution)/shard_map/write/pallas_call | solution.py:409
